TPU v7x, 32 devices: a whole 2x2x4 slice. The times are simulated.
32 devices in a mesh: tm: 16 (over z, x, core), grp: 2 (over y).
Axes of the slice: x: 2, y: 2, z: 4, core: 2. Of those that a mesh axis runs over, the one named last changes fastest.
Arguments:
- residual: float32 [16, 2, 3072], P('tm', 'grp'), may hold values from -6 to 6
- weight: float32 [16, 2, 3072], P('tm', 'grp'), may hold values from 0.25 to 4
- source_part: float32 [5, 16, 2, 3072], P(None, 'tm', 'grp'), may hold values from -2.5 to 2.5
- source_index: int32 [16, 2, 3072], P('tm', 'grp'), may hold values from 0 to 4095
- source_delta: float32 [5, 16, 4096], P(None, 'tm'), may hold values from -6 to 6
- attitude_part: float32 [3, 16, 2, 3072], P(None, 'tm', 'grp'), may hold values from -6 to 6
- spline_phase: float32 [16, 2, 3072], P('tm', 'grp'), may hold values from 0 to 1
- knot_index: int32 [16, 2, 3072], P('tm', 'grp'), may hold values from 0 to 1535, as said below
- calib_part: float32 [6, 16, 2, 3072], P(None, 'tm', 'grp'), may hold values from -6 to 6
- calib_index: int32 [16, 2, 3072], P('tm', 'grp'), may hold values from 0 to 2047
- global_part: float32 [4, 16, 2, 3072], P(None, 'tm', 'grp'), may hold values from -6 to 6
Outputs:
- residual_new: float32 [16, 2, 3072], P('tm', 'grp')
- attitude_step: float32 [3, 1536], P(None, 'tm')
- calib_step: float32 [6, 2048], replicated
- global_step: float32 [4], replicated
Inputs may be any that keep to these rules, and one draw needn't show every extreme that they name: `knot_index`: observation r of interval t (in any group) lies in knot interval t * 96 + 4 * (r // 128) + j for some j in 0 .. 3.
All inputs are finite; a program needn't handle non-finite values.
Results may differ from a plain program's by a relative error of at most 0.00012.
Values sent between devices are 32-bit elements; how exact they have to be, the bound alone decides.
A program may use at most 128 MiB of HBM per device.

v0:
```python
import functools

import jax
import jax.numpy as jnp
from jax import lax
from jax.experimental import pallas as pl
from jax.experimental.pallas import tpu as pltpu
from jax.sharding import PartitionSpec as P

TILE = 128
KPT = 4
UNITS = 2048
CPAR = 6
GPAR = 4
ATT_SWEEPS = 4

OMEGA = 0.6
RIDGE = 1.0
LANES = 128
LOW = 256
HALO = 3 * ATT_SWEEPS
MESH = pl.DeviceIdType.MESH
F32 = jnp.float32
BF16 = jnp.bfloat16

ATT_ROWS = 72
UNIT_ROWS = 24
NORMAL_ROWS = 32


def pairs_of(extent):
    return [(a, b) for a in range(extent) for b in range(a, extent)]


def lane_pick(table, index):
    return lax.gather(
        table,
        index[..., None],
        lax.GatherDimensionNumbers(
            offset_dims=(),
            collapsed_slice_dims=(1,),
            start_index_map=(1,),
            operand_batching_dims=(0,),
            start_indices_batching_dims=(0,),
        ),
        (1, 1),
        mode=lax.GatherScatterMode.PROMISE_IN_BOUNDS,
    )


def spline_basis(phase):
    inverse = 1.0 - phase
    square = phase * phase
    cubed = square * phase
    return [
        inverse * inverse * inverse / 6.0,
        (3.0 * cubed - 6.0 * square + 4.0) / 6.0,
        (-3.0 * cubed + 3.0 * square + 3.0 * phase + 1.0) / 6.0,
        cubed / 6.0,
    ]


def cholesky_lists(matrix, extent):
    lower = [[None] * extent for _ in range(extent)]
    inverse = [None] * extent
    for column in range(extent):
        pivot = matrix[column][column]
        for k in range(column):
            pivot = pivot - lower[column][k] * lower[column][k]
        root = jnp.sqrt(pivot)
        lower[column][column] = root
        inverse[column] = 1.0 / root
        for row in range(column + 1, extent):
            entry = matrix[row][column]
            for k in range(column):
                entry = entry - lower[row][k] * lower[column][k]
            lower[row][column] = entry * inverse[column]
    return lower, inverse


def solve_lower(lower, inverse, vector):
    result = []
    for row in range(len(vector)):
        running = vector[row]
        for k in range(row):
            running = running - lower[row][k] * result[k]
        result.append(running * inverse[row])
    return result


def solve_upper(lower, inverse, vector):
    extent = len(vector)
    result = [None] * extent
    for row in reversed(range(extent)):
        running = vector[row]
        for k in range(row + 1, extent):
            running = running - lower[k][row] * result[k]
        result[row] = running * inverse[row]
    return result


def symmetric(upper, extent):
    matrix = [[None] * extent for _ in range(extent)]
    for position, (a, b) in enumerate(pairs_of(extent)):
        value = upper[position] + (RIDGE if a == b else 0.0)
        matrix[a][b] = value
        matrix[b][a] = value
    return matrix


def split_three(value):
    first = value.astype(BF16).astype(F32)
    rest = value - first
    second = rest.astype(BF16).astype(F32)
    third = (rest - second).astype(BF16).astype(F32)
    return [first, second, third]


def dot_nt(left, right):
    return lax.dot_general(
        left, right, (((1,), (1,)), ((), ())), preferred_element_type=F32
    )


def two_tiles(ref, tile, rows, tiles):
    return jnp.concatenate(
        [ref[pl.ds(tile, rows, stride=tiles), :], ref[pl.ds(tile + 1, rows, stride=tiles), :]],
        axis=1,
    )


def two_rows(ref, tile):
    return jnp.concatenate([ref[pl.ds(tile, 1), :], ref[pl.ds(tile + 1, 1), :]], axis=1)


def one_hot(row, extent):
    spots = lax.broadcasted_iota(jnp.int32, (extent, row.shape[1]), 0)
    return jnp.where(spots == row, 1.0, 0.0).astype(BF16)


def by_high(part, high):
    return jnp.concatenate(
        [jnp.where(high == h, part, 0.0) for h in range(UNITS // LOW)], axis=0
    )


def block_pieces(blocks):
    width = UNITS // blocks
    for piece in range(UNITS // LANES):
        unit = piece * LANES
        yield unit // width, unit % width, unit // LOW, unit % LOW


def first_kernel(
    blocks, res_ref, w_ref, sp_ref, si_ref, sd_ref, ap_ref, ph_ref, kn_ref, cp_ref, ci_ref,
    gp_ref, first_ref, normal_ref, mats_ref, att, cal, acc_att, acc_cal,
):
    tiles = res_ref.shape[0]
    weights = w_ref[...]
    sources = si_ref[...]
    high, low = lax.shift_right_logical(sources, 7), lax.bitwise_and(sources, 127)
    picked = [jnp.zeros((tiles, LANES), F32) for _ in range(5)]
    for row in range(sd_ref.shape[1]):
        here = high == row
        for c in range(5):
            table = jnp.broadcast_to(sd_ref[c, row : row + 1, :], (tiles, LANES))
            picked[c] = jnp.where(here, lane_pick(table, low), picked[c])
    total = sp_ref[0] * picked[0]
    for c in range(1, 5):
        total = total + sp_ref[c] * picked[c]
    first = res_ref[...] - total
    first_ref[...] = first
    basis = spline_basis(ph_ref[...])
    axes = [ap_ref[c] for c in range(3)]
    products = [weights * axes[a] * axes[b] for a, b in pairs_of(3)]
    rights = [weights * axes[a] * first for a in range(3)]
    place = 0
    for i in range(4):
        for d in range(4 - i):
            both = basis[i] * basis[i + d]
            for product in products:
                att[place * tiles : (place + 1) * tiles, :] = both * product
                place += 1
    for i in range(4):
        for right in rights:
            att[place * tiles : (place + 1) * tiles, :] = basis[i] * right
            place += 1
    place = 0
    for a, b in pairs_of(CPAR):
        cal[place * tiles : (place + 1) * tiles, :] = weights * cp_ref[a] * cp_ref[b]
        place += 1
    cal[place * tiles :, :] = jnp.zeros(((UNIT_ROWS - place) * tiles, LANES), F32)
    global_rows = [
        jnp.sum(weights * gp_ref[a] * gp_ref[b], axis=0, keepdims=True)
        for a, b in pairs_of(GPAR)
    ]
    acc_att[...] = jnp.zeros_like(acc_att)
    acc_cal[...] = jnp.zeros_like(acc_cal)
    base = lax.axis_index("tm") * (tiles * KPT)

    def step(no, carry):
        tile = no * 2
        knots = two_rows(kn_ref, tile) - base
        nodes = one_hot(knots, LANES)
        part = acc_att[...]
        for piece in split_three(two_tiles(att, tile, ATT_ROWS, tiles)):
            part = part + dot_nt(piece.astype(BF16), nodes)
        acc_att[...] = part
        units = two_rows(ci_ref, tile)
        upper, lower = lax.shift_right_logical(units, 8), lax.bitwise_and(units, 255)
        spots = one_hot(lower, LOW)
        part = acc_cal[...]
        for piece in split_three(two_tiles(cal, tile, UNIT_ROWS, tiles)):
            part = part + dot_nt(by_high(piece, upper).astype(BF16), spots)
        acc_cal[...] = part
        return carry

    lax.fori_loop(0, tiles // 2, step, 0, unroll=2)
    band = [None] * 5
    place = 0
    for i in range(4):
        for d in list(range(4 - i)):
            rows = acc_att[place : place + 6, :]
            rows = pltpu.roll(rows, i, 1) if i else rows
            band[d] = rows if band[d] is None else band[d] + rows
            place += 6
    for i in range(4):
        rows = acc_att[place : place + 3, :]
        rows = pltpu.roll(rows, i, 1) if i else rows
        band[4] = rows if band[4] is None else band[4] + rows
        place += 3
    for d in range(4):
        normal_ref[d * 6 : (d + 1) * 6, :] = band[d]
    normal_ref[24:27, :] = band[4]
    normal_ref[27:, :] = jnp.zeros((NORMAL_ROWS - 27, LANES), F32)
    mats_ref[...] = jnp.zeros_like(mats_ref)
    for block, at, h, start in block_pieces(blocks):
        mats_ref[block, 0:21, at : at + LANES] = acc_cal[
            h * UNIT_ROWS : h * UNIT_ROWS + 21, start : start + LANES
        ]
        if at == 0:
            for no, row in enumerate(global_rows):
                mats_ref[block, 21 + no : 22 + no, 0:LANES] = row


def attitude_kernel(
    shape, nodes_dev, normal_ref, mats_ref, x_ref, total_ref,
    near, mine, whole, near_s, near_r, mine_s, mine_r, whole_s, whole_r,
):
    count, groups, blocks = shape
    t, g = lax.axis_index("tm"), lax.axis_index("grp")
    has_before, has_after = t > 0, t < count - 1

    def peer_tm(k):
        return lax.rem(t + k, count)

    def peer_grp(k):
        return lax.rem(g + k, groups)

    barrier = pltpu.get_barrier_semaphore()

    def greet(where):
        pl.semaphore_signal(barrier, inc=1, device_id=where, device_id_type=MESH)

    lax.fori_loop(1, count, lambda k, c: (greet({"tm": peer_tm(k), "grp": g}), c)[1], 0)
    for k in range(1, groups):
        greet({"tm": t, "grp": peer_grp(k)})
        greet({"tm": peer_tm(1), "grp": peer_grp(k)})
        greet({"tm": peer_tm(count - 1), "grp": peer_grp(k)})
    pl.semaphore_wait(barrier, count - 1 + 3 * (groups - 1))

    def near_copy(offset, k):
        slot = (1 - offset) * groups + g
        return pltpu.make_async_remote_copy(
            src_ref=normal_ref,
            dst_ref=near.at[slot],
            send_sem=near_s.at[(offset + 1) * groups + k],
            recv_sem=near_r.at[slot],
            device_id={"tm": t + offset, "grp": peer_grp(k)},
            device_id_type=MESH,
        )

    def near_arrival(offset, k):
        slot = (offset + 1) * groups + peer_grp(k)
        return pltpu.make_async_remote_copy(
            src_ref=normal_ref,
            dst_ref=near.at[slot],
            send_sem=near_s.at[(offset + 1) * groups + k],
            recv_sem=near_r.at[slot],
            device_id={"tm": t + offset, "grp": peer_grp(k)},
            device_id_type=MESH,
        )

    def each_near(do):
        for k in range(1, groups):
            do(0, k)

        @pl.when(has_before)
        def _():
            for k in range(groups):
                do(-1, k)

        @pl.when(has_after)
        def _():
            for k in range(groups):
                do(1, k)

    each_near(lambda offset, k: near_copy(offset, k).start())

    def whole_copy(k):
        p = peer_tm(k)
        return pltpu.make_async_remote_copy(
            src_ref=mats_ref.at[lax.rem(p, blocks)],
            dst_ref=whole.at[t],
            send_sem=whole_s.at[k],
            recv_sem=whole_r.at[t],
            device_id={"tm": p, "grp": g},
            device_id_type=MESH,
        )

    def whole_arrival(k):
        p = peer_tm(k)
        return pltpu.make_async_remote_copy(
            src_ref=mats_ref.at[lax.rem(p, blocks)],
            dst_ref=whole.at[p],
            send_sem=whole_s.at[k],
            recv_sem=whole_r.at[p],
            device_id={"tm": p, "grp": g},
            device_id_type=MESH,
        )

    lax.fori_loop(1, count, lambda k, c: (whole_copy(k).start(), c)[1], 0)
    whole[t] = mats_ref[lax.rem(t, blocks)]
    near[groups + g] = normal_ref[...]

    @pl.when(jnp.logical_not(has_before))
    def _():
        near[0:groups] = jnp.zeros((groups, NORMAL_ROWS, LANES), F32)

    @pl.when(jnp.logical_not(has_after))
    def _():
        near[2 * groups :] = jnp.zeros((groups, NORMAL_ROWS, LANES), F32)

    each_near(lambda offset, k: near_arrival(offset, k).wait_recv())
    sums = []
    for s in range(3):
        part = near[s * groups]
        for q in range(1, groups):
            part = part + near[s * groups + q]
        sums.append(part)
    lane = lax.broadcasted_iota(jnp.int32, (NORMAL_ROWS, LANES), 1)
    before = pltpu.roll(sums[0], (HALO - nodes_dev) % LANES, 1)
    own = pltpu.roll(sums[1], HALO, 1)
    after = pltpu.roll(sums[2], (HALO + nodes_dev) % LANES, 1)
    end = nodes_dev + HALO
    normals = (
        own
        + jnp.where((lane >= 3) & (lane < HALO + 3), before, 0.0)
        + jnp.where((lane >= end) & (lane < end + HALO), after, 0.0)
    )
    spot = lax.broadcasted_iota(jnp.int32, (1, LANES), 1)
    exists = (spot >= jnp.where(has_before, 0, HALO)) & (
        spot < jnp.where(has_after, LANES, end)
    )
    normals = jnp.where(exists, normals, 0.0)
    index = {}
    for position, (a, b) in enumerate(pairs_of(3)):
        index[a, b] = index[b, a] = position
    band = [[normals[d * 6 + p : d * 6 + p + 1, :] for p in range(6)] for d in range(4)]
    right = [normals[24 + c : 25 + c, :] for c in range(3)]
    lower, inverse = cholesky_lists(symmetric(band[0], 3), 3)

    def precondition(vector):
        return solve_upper(lower, inverse, solve_lower(lower, inverse, vector))

    x = [OMEGA * value for value in precondition(right)]
    for _ in range(1, ATT_SWEEPS):
        out = [right[c] - x[c] for c in range(3)]
        for d in range(4):
            ahead = [pltpu.roll(x[c], LANES - d, 1) for c in range(3)] if d else x
            for a in range(3):
                for b in range(3):
                    out[a] = out[a] - band[d][index[a, b]] * ahead[b]
        for d in range(1, 4):
            for a in range(3):
                term = band[d][index[a, 0]] * x[0]
                for b in range(1, 3):
                    term = term + band[d][index[a, b]] * x[b]
                out[a] = out[a] - pltpu.roll(term, d, 1)
        change = precondition(out)
        x = [jnp.where(exists, x[c] + OMEGA * change[c], 0.0) for c in range(3)]
    x_ref[...] = jnp.zeros_like(x_ref)
    for c in range(3):
        x_ref[c : c + 1, :] = x[c]
        scaled = lower[c][c] * x[c]
        for k in range(c + 1, 3):
            scaled = scaled + lower[k][c] * x[k]
        x_ref[3 + c : 4 + c, :] = pltpu.roll(scaled, LANES - HALO, 1)

    lax.fori_loop(1, count, lambda k, c: (whole_arrival(k).wait_recv(), c)[1], 0)
    mine[g] = lax.fori_loop(1, count, lambda k, c: c + whole[k], whole[0])

    def mine_copy(k):
        return pltpu.make_async_remote_copy(
            src_ref=mine.at[g],
            dst_ref=mine.at[g],
            send_sem=mine_s.at[k],
            recv_sem=mine_r.at[g],
            device_id={"tm": t, "grp": peer_grp(k)},
            device_id_type=MESH,
        )

    def mine_arrival(k):
        q = peer_grp(k)
        return pltpu.make_async_remote_copy(
            src_ref=mine.at[q],
            dst_ref=mine.at[q],
            send_sem=mine_s.at[k],
            recv_sem=mine_r.at[q],
            device_id={"tm": t, "grp": q},
            device_id_type=MESH,
        )

    for k in range(1, groups):
        mine_copy(k).start()
    for k in range(1, groups):
        mine_arrival(k).wait_recv()
    total = mine[0]
    for q in range(1, groups):
        total = total + mine[q]
    total_ref[...] = total
    for k in range(1, groups):
        mine_copy(k).wait_send()
    each_near(lambda offset, k: near_copy(offset, k).wait_send())
    lax.fori_loop(1, count, lambda k, c: (whole_copy(k).wait_send(), c)[1], 0)


def second_kernel(
    blocks, first_ref, x_ref, w_ref, ap_ref, ph_ref, kn_ref, cp_ref, ci_ref, gp_ref,
    second_ref, rhs_ref, step_ref, cal, acc,
):
    tiles = first_ref.shape[0]
    nodes_dev = tiles * KPT
    weights = w_ref[...]
    base = lax.axis_index("tm") * nodes_dev
    local = kn_ref[...] - base + HALO
    basis = spline_basis(ph_ref[...])
    tables = [jnp.broadcast_to(x_ref[c : c + 1, :], (tiles, LANES)) for c in range(3)]
    second = first_ref[...]
    for i in range(4):
        moved = ap_ref[0] * lane_pick(tables[0], local + i)
        for c in range(1, 3):
            moved = moved + ap_ref[c] * lane_pick(tables[c], local + i)
        second = second - basis[i] * moved
    second_ref[...] = second
    step_ref[...] = x_ref[3:6, 0:nodes_dev]
    weighted = weights * second
    for a in range(CPAR):
        cal[a * tiles : (a + 1) * tiles, :] = weighted * cp_ref[a]
    cal[CPAR * tiles :, :] = jnp.zeros(((8 - CPAR) * tiles, LANES), F32)
    sums = [jnp.sum(weighted * gp_ref[a], axis=0, keepdims=True) for a in range(GPAR)]
    acc[...] = jnp.zeros_like(acc)

    def step(no, carry):
        tile = no * 2
        units = two_rows(ci_ref, tile)
        upper, lower = lax.shift_right_logical(units, 8), lax.bitwise_and(units, 255)
        pieces = [by_high(p, upper) for p in split_three(two_tiles(cal, tile, 8, tiles))]
        lhs = jnp.concatenate(pieces, axis=0).astype(BF16)
        acc[...] = acc[...] + dot_nt(lhs, one_hot(lower, LOW))
        return carry

    lax.fori_loop(0, tiles // 2, step, 0, unroll=2)
    rows = 8 * (UNITS // LOW)
    total = acc[0:rows, :] + acc[rows : 2 * rows, :] + acc[2 * rows : 3 * rows, :]
    lane = lax.broadcasted_iota(jnp.int32, (1, LANES), 1)
    folded = [row + pltpu.roll(row, LANES // 2, 1) for row in sums]
    packed = [jnp.where(lane < LANES // 2, folded[2 * k], folded[2 * k + 1]) for k in range(2)]
    if rhs_ref.shape[2] > LANES:
        rhs_ref[...] = jnp.zeros_like(rhs_ref)
    for block, at, h, start in block_pieces(blocks):
        rhs_ref[block, 0:CPAR, at : at + LANES] = total[
            h * 8 : h * 8 + CPAR, start : start + LANES
        ]
        if at == 0:
            for k in range(2):
                rhs_ref[block, CPAR + k : CPAR + k + 1, 0:LANES] = packed[k]


def solve_kernel(
    shape, rhs_ref, total_ref, out_ref, glob_ref,
    whole, mine, ready, spread, whole_s, whole_r, mine_s, mine_r, spread_s, spread_r,
):
    count, groups, blocks = shape
    width = rhs_ref.shape[2]
    t, g = lax.axis_index("tm"), lax.axis_index("grp")
    block = lax.rem(t, blocks)
    family = t - block

    def peer_tm(k):
        return lax.rem(t + k, count)

    def peer_grp(k):
        return lax.rem(g + k, groups)

    barrier = pltpu.get_barrier_semaphore()

    def greet(where):
        pl.semaphore_signal(barrier, inc=1, device_id=where, device_id_type=MESH)

    lax.fori_loop(1, count, lambda k, c: (greet({"tm": peer_tm(k), "grp": g}), c)[1], 0)
    for k in range(1, groups):
        greet({"tm": t, "grp": peer_grp(k)})
    pl.semaphore_wait(barrier, count - 1 + groups - 1)

    def whole_copy(k, slot):
        p = peer_tm(k)
        return pltpu.make_async_remote_copy(
            src_ref=rhs_ref.at[lax.rem(p, blocks)],
            dst_ref=whole.at[slot],
            send_sem=whole_s.at[k],
            recv_sem=whole_r.at[slot],
            device_id={"tm": p, "grp": g},
            device_id_type=MESH,
        )

    lax.fori_loop(1, count, lambda k, c: (whole_copy(k, t).start(), c)[1], 0)
    whole[t] = rhs_ref[block]
    matrix = [total_ref[p : p + 1, :] for p in range(21)]
    lower, inverse = cholesky_lists(symmetric(matrix, CPAR), CPAR)
    upper_g = [
        jnp.broadcast_to(
            jnp.sum(total_ref[21 + p : 22 + p, 0:LANES], axis=1, keepdims=True), (1, LANES)
        )
        for p in range(10)
    ]
    lower_g, inverse_g = cholesky_lists(symmetric(upper_g, GPAR), GPAR)
    lax.fori_loop(1, count, lambda k, c: (whole_copy(k, peer_tm(k)).wait_recv(), c)[1], 0)
    mine[g] = lax.fori_loop(1, count, lambda k, c: c + whole[k], whole[0])

    def mine_copy(k, slot):
        return pltpu.make_async_remote_copy(
            src_ref=mine.at[slot],
            dst_ref=mine.at[slot],
            send_sem=mine_s.at[k],
            recv_sem=mine_r.at[slot],
            device_id={"tm": t, "grp": peer_grp(k)},
            device_id_type=MESH,
        )

    for k in range(1, groups):
        mine_copy(k, g).start()
    for k in range(1, groups):
        mine_copy(k, peer_grp(k)).wait_recv()
    total = mine[0]
    for q in range(1, groups):
        total = total + mine[q]
    right = [total[c : c + 1, :] for c in range(CPAR)]
    white = solve_lower(lower, inverse, right)
    solved = solve_upper(lower, inverse, white)
    for c in range(CPAR):
        ready[c : c + 1, :] = white[c]
        ready[CPAR + c : CPAR + c + 1, :] = solved[c]
    ready[2 * CPAR :, :] = jnp.zeros((16 - 2 * CPAR, width), F32)

    def spread_copy(k, slot):
        return pltpu.make_async_remote_copy(
            src_ref=ready,
            dst_ref=spread.at[slot],
            send_sem=spread_s.at[k],
            recv_sem=spread_r.at[slot],
            device_id={"tm": family + lax.rem(block + k, blocks), "grp": g},
            device_id_type=MESH,
        )

    lax.fori_loop(1, blocks, lambda k, c: (spread_copy(k, block).start(), c)[1], 0)
    spread[block] = ready[...]
    lane = lax.broadcasted_iota(jnp.int32, (1, LANES), 1)
    right_g = []
    for c in range(GPAR):
        row = total[CPAR + c // 2 : CPAR + c // 2 + 1, 0:LANES]
        half = (lane < LANES // 2) if c % 2 == 0 else (lane >= LANES // 2)
        value = jnp.sum(jnp.where(half, row, 0.0), axis=1, keepdims=True)
        right_g.append(jnp.broadcast_to(value, (1, LANES)))
    white_g = solve_lower(lower_g, inverse_g, right_g)
    solved_g = solve_upper(lower_g, inverse_g, white_g)
    for c in range(GPAR):
        glob_ref[c : c + 1, :] = white_g[c]
        glob_ref[GPAR + c : GPAR + c + 1, :] = solved_g[c]
    lax.fori_loop(
        1,
        blocks,
        lambda k, c: (spread_copy(k, lax.rem(block + k, blocks)).wait_recv(), c)[1],
        0,
    )
    out_ref[...] = spread[...]
    lax.fori_loop(1, count, lambda k, c: (whole_copy(k, t).wait_send(), c)[1], 0)
    for k in range(1, groups):
        mine_copy(k, g).wait_send()
    lax.fori_loop(1, blocks, lambda k, c: (spread_copy(k, block).wait_send(), c)[1], 0)


def final_kernel(
    blocks, second_ref, solved_ref, glob_ref, cp_ref, ci_ref, gp_ref, res_ref, step_ref
):
    tiles = second_ref.shape[0]
    units = ci_ref[...]
    high, low = lax.shift_right_logical(units, 7), lax.bitwise_and(units, 127)
    picked = [jnp.zeros((tiles, LANES), F32) for _ in range(CPAR)]
    width = UNITS // blocks
    for row in range(UNITS // LANES):
        block, at = (row * LANES) // width, (row * LANES) % width
        here = high == row
        step_ref[:, row * LANES : (row + 1) * LANES] = solved_ref[block, 0:CPAR, at : at + LANES]
        for c in range(CPAR):
            line = solved_ref[block, CPAR + c : CPAR + c + 1, at : at + LANES]
            table = jnp.broadcast_to(line, (tiles, LANES))
            picked[c] = jnp.where(here, lane_pick(table, low), picked[c])
    out = second_ref[...]
    for c in range(CPAR):
        out = out - cp_ref[c] * picked[c]
    for c in range(GPAR):
        out = out - gp_ref[c] * glob_ref[GPAR + c : GPAR + c + 1, :]
    res_ref[...] = out


def per_device(
    shape, residual, weight, source_part, source_index, source_delta, attitude_part,
    spline_phase, knot_index, calib_part, calib_index, global_part,
):
    count, groups, blocks = shape
    row_count = residual.shape[-1]
    tiles = row_count // TILE
    nodes_dev = tiles * KPT
    width = UNITS // blocks

    def flat(value):
        return value.reshape(tiles, TILE)

    def deep(value):
        return value.reshape(value.shape[0], -1, LANES)

    weights, phase, knots, units = map(flat, (weight, spline_phase, knot_index, calib_index))
    axes, calib, glob = map(deep, (attitude_part, calib_part, global_part))

    def out(*dims):
        return jax.ShapeDtypeStruct(dims, F32)

    dma = pltpu.SemaphoreType.DMA
    first, normals, mats = pl.pallas_call(
        functools.partial(first_kernel, blocks),
        out_shape=(
            out(tiles, LANES), out(NORMAL_ROWS, LANES), out(blocks, NORMAL_ROWS, width),
        ),
        scratch_shapes=[
            pltpu.VMEM((ATT_ROWS * tiles, LANES), F32),
            pltpu.VMEM((UNIT_ROWS * tiles, LANES), F32),
            pltpu.VMEM((ATT_ROWS, LANES), F32),
            pltpu.VMEM((UNIT_ROWS * (UNITS // LOW), LOW), F32),
        ],
        name="first",
    )(
        flat(residual), weights, deep(source_part), flat(source_index), deep(source_delta),
        axes, phase, knots, calib, units, glob,
    )
    x, total = pl.pallas_call(
        functools.partial(attitude_kernel, shape, nodes_dev),
        out_shape=(out(8, LANES), out(NORMAL_ROWS, width)),
        scratch_shapes=[
            pltpu.VMEM((3 * groups, NORMAL_ROWS, LANES), F32),
            pltpu.VMEM((groups, NORMAL_ROWS, width), F32),
            pltpu.VMEM((count, NORMAL_ROWS, width), F32),
            dma((3 * groups,)), dma((3 * groups,)),
            dma((groups,)), dma((groups,)),
            dma((count,)), dma((count,)),
        ],
        in_specs=[pl.BlockSpec(memory_space=pltpu.VMEM)] * 2,
        compiler_params=pltpu.CompilerParams(collective_id=0, has_side_effects=True),
        name="attitude",
    )(normals, mats)
    second, rhs, attitude_step = pl.pallas_call(
        functools.partial(second_kernel, blocks),
        out_shape=(out(tiles, LANES), out(blocks, 8, width), out(3, nodes_dev)),
        scratch_shapes=[
            pltpu.VMEM((8 * tiles, LANES), F32),
            pltpu.VMEM((3 * 8 * (UNITS // LOW), LOW), F32),
        ],
        name="second",
    )(first, x, weights, axes, phase, knots, calib, units, glob)
    solved, global_out = pl.pallas_call(
        functools.partial(solve_kernel, shape),
        out_shape=(out(blocks, 16, width), out(2 * GPAR, LANES)),
        scratch_shapes=[
            pltpu.VMEM((count, 8, width), F32),
            pltpu.VMEM((groups, 8, width), F32),
            pltpu.VMEM((16, width), F32),
            pltpu.VMEM((blocks, 16, width), F32),
            dma((count,)), dma((count,)),
            dma((groups,)), dma((groups,)),
            dma((blocks,)), dma((blocks,)),
        ],
        in_specs=[pl.BlockSpec(memory_space=pltpu.VMEM)] * 2,
        compiler_params=pltpu.CompilerParams(collective_id=1, has_side_effects=True),
        name="solve",
    )(rhs, total)
    final, calib_step = pl.pallas_call(
        functools.partial(final_kernel, blocks),
        out_shape=(out(tiles, LANES), out(CPAR, UNITS)),
        name="final",
    )(second, solved, global_out, calib, units, glob)
    return final.reshape(residual.shape), attitude_step, calib_step, global_out[:GPAR, 0]


def solution(mesh):
    count, groups = mesh.shape["tm"], mesh.shape["grp"]
    blocks = min(count, UNITS // LANES)
    return jax.shard_map(
        functools.partial(per_device, (count, groups, blocks)),
        mesh=mesh,
        in_specs=(
            P("tm", "grp", None),
            P("tm", "grp", None),
            P(None, "tm", "grp", None),
            P("tm", "grp", None),
            P(None, "tm", None),
            P(None, "tm", "grp", None),
            P("tm", "grp", None),
            P("tm", "grp", None),
            P(None, "tm", "grp", None),
            P("tm", "grp", None),
            P(None, "tm", "grp", None),
        ),
        out_specs=(P("tm", "grp", None), P(None, "tm"), P(), P()),
        check_vma=False,
    )
```

profile of v0, /device:TPU:0, one launch (start us, length us, event | category | flops | bytes accessed | tf_op | source)
XLA Modules:
  0.0 48.2 jit_solution(10883075231204080065)
XLA Ops:
  0.6 6.3 %first.1 = (f32[24,128]{1,0:T(8,128)}, f32[32,128]{1,0:T(8,128)}, f32[16,32,128]{2,1,0:T(8,128)}) custom-call(f32[24,128]{1,0:T(8,128)} %bitcast.31, f32[24,128]{1,0:T(8,128)} %bitcast.25, f32[5,24,128]{2,1,0:T(8,128)} %bitcast.24, s32[24,128]{1,0:T(8,128)} %bitcast.32, f32[5,32,128]{2,1,0:T(8,128)} %bitcast.23, f32[3,24,128]{2,1,0:T(8,128)} %bitcast.18, ...), custom_call_target="tpu_custom_call" | custom-call | tf_op jit(solution)/shard_map/first/pallas_call | solution.py:650
  6.9 16.9 %attitude.1 = (f32[8,128]{1,0:T(8,128)}, f32[32,128]{1,0:T(8,128)}) custom-call(f32[32,128]{1,0:T(8,128)} %get-tuple-element.17.normal_ref, f32[16,32,128]{2,1,0:T(8,128)} %get-tuple-element.18.mats_ref), custom_call_target="tpu_custom_call" | custom-call | tf_op jit(solution)/shard_map/attitude/pallas_call | solution.py:666
  23.8 3.6 %second.1 = (f32[24,128]{1,0:T(8,128)}, f32[16,8,128]{2,1,0:T(8,128)}, f32[3,96]{1,0:T(4,128)}) custom-call(f32[24,128]{1,0:T(8,128)} %get-tuple-element.16.first_ref, f32[8,128]{1,0:T(8,128)} %get-tuple-element.19.x_ref, f32[24,128]{1,0:T(8,128)} %bitcast.26, f32[3,24,128]{2,1,0:T(8,128)} %bitcast.19, f32[24,128]{1,0:T(8,128)} %bitcast.28, ...), custom_call_target="tpu_custom_call" | custom-call | tf_op jit(solution)/shard_map/second/pallas_call | solution.py:681
  27.4 17.8 %solve.1 = (f32[16,16,128]{2,1,0:T(8,128)}, f32[8,128]{1,0:T(8,128)}) custom-call(f32[16,8,128]{2,1,0:T(8,128)} %get-tuple-element.21.rhs_ref, f32[32,128]{1,0:T(8,128)} %get-tuple-element.22.total_ref), custom_call_target="tpu_custom_call" | custom-call | tf_op jit(solution)/shard_map/solve/pallas_call | solution.py:690
  45.2 0.0 copy-start
  45.2 2.4 %final.1 = (f32[24,128]{1,0:T(8,128)}, f32[6,2048]{1,0:T(8,128)}) custom-call(f32[24,128]{1,0:T(8,128)} %get-tuple-element.20.second_ref, f32[16,16,128]{2,1,0:T(8,128)} %get-tuple-element.23.solved_ref, f32[8,128]{1,0:T(8,128)} %get-tuple-element.24.glob_ref, f32[6,24,128]{2,1,0:T(8,128)} %bitcast.14, s32[24,128]{1,0:T(8,128)} %bitcast.22, ...), custom_call_target="tpu_custom_call" | custom-call | tf_op jit(solution)/shard_map/final/pallas_call | solution.py:706
  47.6 0.0 copy-done
  47.6 0.6 %slice_reduce_fusion = f32[4]{0:T(128)} fusion(f32[8,128]{1,0:T(8,128)S(1)} %copy-done), kind=kLoop, calls=%fused_computation | loop fusion | bytes 32 | tf_op jit(solution)/shard_map/slice | solution.py:711
Async XLA Ops:
  45.2 2.4 %copy-start = (f32[8,128]{1,0:T(8,128)S(1)}, f32[8,128]{1,0:T(8,128)}, u32[]{:S(2)}) copy-start(f32[8,128]{1,0:T(8,128)} %get-tuple-element.24.glob_ref) | copy-start | bytes 12292
where the time goes:
time: 48.5 us; the launch traced here: 48.2 us
  Pallas kernels  46.9 us (97%)
  between operations  0.66 us (1%)
  local copies, waits for them, and re-layouts  0.63 us (1%)
    pallas_call x1, Pallas kernels, per_device(): pl.pallas_call(functools.partial(solve_kernel, shape), out_shape=(out(blo...  17.8 us
    pallas_call x1, Pallas kernels, per_device(): pl.pallas_call(functools.partial(attitude_kernel, shape, nodes_dev), out_...  16.9 us
    pallas_call x1, Pallas kernels, per_device(): pl.pallas_call(functools.partial(first_kernel, blocks), out_shape=(out(ti...  6.27 us
    pallas_call x1, Pallas kernels, per_device(): pl.pallas_call(functools.partial(second_kernel, blocks), out_shape=(out(t...  3.62 us
    pallas_call x1, Pallas kernels, per_device(): pl.pallas_call(functools.partial(final_kernel, blocks), out_shape=(out(ti...  2.36 us

commit v1 on v0

--- a/solution.py
+++ b/solution.py
@@ -151,10 +151,34 @@
         yield unit // width, unit % width, unit // LOW, unit % LOW
 
 
-def first_kernel(
-    blocks, res_ref, w_ref, sp_ref, si_ref, sd_ref, ap_ref, ph_ref, kn_ref, cp_ref, ci_ref,
-    gp_ref, first_ref, normal_ref, mats_ref, att, cal, acc_att, acc_cal,
+def step_kernel(
+    shape, nodes_dev, res_ref, w_ref, sp_ref, si_ref, sd_ref, ap_ref, ph_ref, kn_ref, cp_ref,
+    ci_ref, gp_ref, second_ref, step_ref, out_ref, glob_ref,
+    att, cal, rcal, acc_att, acc_cal, acc_rhs, normal_ref, mats_ref, rhs_ref,
+    near, mine, whole, rwhole, rmine, ready, spread,
+    near_s, near_r, mine_s, mine_r, whole_s, whole_r,
+    rwhole_s, rwhole_r, rmine_s, rmine_r, spread_s, spread_r,
 ):
+    count, groups, blocks = shape
+    t, g = lax.axis_index("tm"), lax.axis_index("grp")
+    has_before, has_after = t > 0, t < count - 1
+
+    def peer_tm(k):
+        return lax.rem(t + k, count)
+
+    def peer_grp(k):
+        return lax.rem(g + k, groups)
+
+    barrier = pltpu.get_barrier_semaphore()
+
+    def greet(where):
+        pl.semaphore_signal(barrier, inc=1, device_id=where, device_id_type=MESH)
+
+    lax.fori_loop(1, count, lambda k, c: (greet({"tm": peer_tm(k), "grp": g}), c)[1], 0)
+    for k in range(1, groups):
+        greet({"tm": t, "grp": peer_grp(k)})
+        greet({"tm": peer_tm(1), "grp": peer_grp(k)})
+        greet({"tm": peer_tm(count - 1), "grp": peer_grp(k)})
     tiles = res_ref.shape[0]
     weights = w_ref[...]
     sources = si_ref[...]
@@ -169,7 +193,6 @@
     for c in range(1, 5):
         total = total + sp_ref[c] * picked[c]
     first = res_ref[...] - total
-    first_ref[...] = first
     basis = spline_basis(ph_ref[...])
     axes = [ap_ref[c] for c in range(3)]
     products = [weights * axes[a] * axes[b] for a, b in pairs_of(3)]
@@ -185,20 +208,10 @@
         for right in rights:
             att[place * tiles : (place + 1) * tiles, :] = basis[i] * right
             place += 1
-    place = 0
-    for a, b in pairs_of(CPAR):
-        cal[place * tiles : (place + 1) * tiles, :] = weights * cp_ref[a] * cp_ref[b]
-        place += 1
-    cal[place * tiles :, :] = jnp.zeros(((UNIT_ROWS - place) * tiles, LANES), F32)
-    global_rows = [
-        jnp.sum(weights * gp_ref[a] * gp_ref[b], axis=0, keepdims=True)
-        for a, b in pairs_of(GPAR)
-    ]
     acc_att[...] = jnp.zeros_like(acc_att)
-    acc_cal[...] = jnp.zeros_like(acc_cal)
     base = lax.axis_index("tm") * (tiles * KPT)
 
-    def step(no, carry):
+    def bin_nodes(no, carry):
         tile = no * 2
         knots = two_rows(kn_ref, tile) - base
         nodes = one_hot(knots, LANES)
@@ -206,16 +219,9 @@
         for piece in split_three(two_tiles(att, tile, ATT_ROWS, tiles)):
             part = part + dot_nt(piece.astype(BF16), nodes)
         acc_att[...] = part
-        units = two_rows(ci_ref, tile)
-        upper, lower = lax.shift_right_logical(units, 8), lax.bitwise_and(units, 255)
-        spots = one_hot(lower, LOW)
-        part = acc_cal[...]
-        for piece in split_three(two_tiles(cal, tile, UNIT_ROWS, tiles)):
-            part = part + dot_nt(by_high(piece, upper).astype(BF16), spots)
-        acc_cal[...] = part
         return carry
 
-    lax.fori_loop(0, tiles // 2, step, 0, unroll=2)
+    lax.fori_loop(0, tiles // 2, bin_nodes, 0, unroll=2)
     band = [None] * 5
     place = 0
     for i in range(4):
@@ -233,6 +239,69 @@
         normal_ref[d * 6 : (d + 1) * 6, :] = band[d]
     normal_ref[24:27, :] = band[4]
     normal_ref[27:, :] = jnp.zeros((NORMAL_ROWS - 27, LANES), F32)
+    pl.semaphore_wait(barrier, count - 1 + 3 * (groups - 1))
+
+    def near_copy(offset, k):
+        slot = (1 - offset) * groups + g
+        return pltpu.make_async_remote_copy(
+            src_ref=normal_ref,
+            dst_ref=near.at[slot],
+            send_sem=near_s.at[(offset + 1) * groups + k],
+            recv_sem=near_r.at[slot],
+            device_id={"tm": t + offset, "grp": peer_grp(k)},
+            device_id_type=MESH,
+        )
+
+    def near_arrival(offset, k):
+        slot = (offset + 1) * groups + peer_grp(k)
+        return pltpu.make_async_remote_copy(
+            src_ref=normal_ref,
+            dst_ref=near.at[slot],
+            send_sem=near_s.at[(offset + 1) * groups + k],
+            recv_sem=near_r.at[slot],
+            device_id={"tm": t + offset, "grp": peer_grp(k)},
+            device_id_type=MESH,
+        )
+
+    def each_near(do):
+        for k in range(1, groups):
+            do(0, k)
+
+        @pl.when(has_before)
+        def _():
+            for k in range(groups):
+                do(-1, k)
+
+        @pl.when(has_after)
+        def _():
+            for k in range(groups):
+                do(1, k)
+
+    each_near(lambda offset, k: near_copy(offset, k).start())
+
+    place = 0
+    for a, b in pairs_of(CPAR):
+        cal[place * tiles : (place + 1) * tiles, :] = weights * cp_ref[a] * cp_ref[b]
+        place += 1
+    cal[place * tiles :, :] = jnp.zeros(((UNIT_ROWS - place) * tiles, LANES), F32)
+    global_rows = [
+        jnp.sum(weights * gp_ref[a] * gp_ref[b], axis=0, keepdims=True)
+        for a, b in pairs_of(GPAR)
+    ]
+    acc_cal[...] = jnp.zeros_like(acc_cal)
+
+    def bin_units(no, carry):
+        tile = no * 2
+        units = two_rows(ci_ref, tile)
+        upper, lower = lax.shift_right_logical(units, 8), lax.bitwise_and(units, 255)
+        spots = one_hot(lower, LOW)
+        part = acc_cal[...]
+        for piece in split_three(two_tiles(cal, tile, UNIT_ROWS, tiles)):
+            part = part + dot_nt(by_high(piece, upper).astype(BF16), spots)
+        acc_cal[...] = part
+        return carry
+
+    lax.fori_loop(0, tiles // 2, bin_units, 0, unroll=2)
     mats_ref[...] = jnp.zeros_like(mats_ref)
     for block, at, h, start in block_pieces(blocks):
         mats_ref[block, 0:21, at : at + LANES] = acc_cal[
@@ -241,71 +310,6 @@
         if at == 0:
             for no, row in enumerate(global_rows):
                 mats_ref[block, 21 + no : 22 + no, 0:LANES] = row
-
-
-def attitude_kernel(
-    shape, nodes_dev, normal_ref, mats_ref, x_ref, total_ref,
-    near, mine, whole, near_s, near_r, mine_s, mine_r, whole_s, whole_r,
-):
-    count, groups, blocks = shape
-    t, g = lax.axis_index("tm"), lax.axis_index("grp")
-    has_before, has_after = t > 0, t < count - 1
-
-    def peer_tm(k):
-        return lax.rem(t + k, count)
-
-    def peer_grp(k):
-        return lax.rem(g + k, groups)
-
-    barrier = pltpu.get_barrier_semaphore()
-
-    def greet(where):
-        pl.semaphore_signal(barrier, inc=1, device_id=where, device_id_type=MESH)
-
-    lax.fori_loop(1, count, lambda k, c: (greet({"tm": peer_tm(k), "grp": g}), c)[1], 0)
-    for k in range(1, groups):
-        greet({"tm": t, "grp": peer_grp(k)})
-        greet({"tm": peer_tm(1), "grp": peer_grp(k)})
-        greet({"tm": peer_tm(count - 1), "grp": peer_grp(k)})
-    pl.semaphore_wait(barrier, count - 1 + 3 * (groups - 1))
-
-    def near_copy(offset, k):
-        slot = (1 - offset) * groups + g
-        return pltpu.make_async_remote_copy(
-            src_ref=normal_ref,
-            dst_ref=near.at[slot],
-            send_sem=near_s.at[(offset + 1) * groups + k],
-            recv_sem=near_r.at[slot],
-            device_id={"tm": t + offset, "grp": peer_grp(k)},
-            device_id_type=MESH,
-        )
-
-    def near_arrival(offset, k):
-        slot = (offset + 1) * groups + peer_grp(k)
-        return pltpu.make_async_remote_copy(
-            src_ref=normal_ref,
-            dst_ref=near.at[slot],
-            send_sem=near_s.at[(offset + 1) * groups + k],
-            recv_sem=near_r.at[slot],
-            device_id={"tm": t + offset, "grp": peer_grp(k)},
-            device_id_type=MESH,
-        )
-
-    def each_near(do):
-        for k in range(1, groups):
-            do(0, k)
-
-        @pl.when(has_before)
-        def _():
-            for k in range(groups):
-                do(-1, k)
-
-        @pl.when(has_after)
-        def _():
-            for k in range(groups):
-                do(1, k)
-
-    each_near(lambda offset, k: near_copy(offset, k).start())
 
     def whole_copy(k):
         p = peer_tm(k)
@@ -389,90 +393,42 @@
                 out[a] = out[a] - pltpu.roll(term, d, 1)
         change = precondition(out)
         x = [jnp.where(exists, x[c] + OMEGA * change[c], 0.0) for c in range(3)]
-    x_ref[...] = jnp.zeros_like(x_ref)
     for c in range(3):
-        x_ref[c : c + 1, :] = x[c]
         scaled = lower[c][c] * x[c]
         for k in range(c + 1, 3):
             scaled = scaled + lower[k][c] * x[k]
-        x_ref[3 + c : 4 + c, :] = pltpu.roll(scaled, LANES - HALO, 1)
-
-    lax.fori_loop(1, count, lambda k, c: (whole_arrival(k).wait_recv(), c)[1], 0)
-    mine[g] = lax.fori_loop(1, count, lambda k, c: c + whole[k], whole[0])
-
-    def mine_copy(k):
-        return pltpu.make_async_remote_copy(
-            src_ref=mine.at[g],
-            dst_ref=mine.at[g],
-            send_sem=mine_s.at[k],
-            recv_sem=mine_r.at[g],
-            device_id={"tm": t, "grp": peer_grp(k)},
-            device_id_type=MESH,
-        )
-
-    def mine_arrival(k):
-        q = peer_grp(k)
-        return pltpu.make_async_remote_copy(
-            src_ref=mine.at[q],
-            dst_ref=mine.at[q],
-            send_sem=mine_s.at[k],
-            recv_sem=mine_r.at[q],
-            device_id={"tm": t, "grp": q},
-            device_id_type=MESH,
-        )
-
-    for k in range(1, groups):
-        mine_copy(k).start()
-    for k in range(1, groups):
-        mine_arrival(k).wait_recv()
-    total = mine[0]
-    for q in range(1, groups):
-        total = total + mine[q]
-    total_ref[...] = total
-    for k in range(1, groups):
-        mine_copy(k).wait_send()
-    each_near(lambda offset, k: near_copy(offset, k).wait_send())
-    lax.fori_loop(1, count, lambda k, c: (whole_copy(k).wait_send(), c)[1], 0)
-
-
-def second_kernel(
-    blocks, first_ref, x_ref, w_ref, ap_ref, ph_ref, kn_ref, cp_ref, ci_ref, gp_ref,
-    second_ref, rhs_ref, step_ref, cal, acc,
-):
-    tiles = first_ref.shape[0]
-    nodes_dev = tiles * KPT
-    weights = w_ref[...]
-    base = lax.axis_index("tm") * nodes_dev
+        moved = pltpu.roll(scaled, LANES - HALO, 1)
+        step_ref[c : c + 1, :] = moved[:, 0:nodes_dev]
+
+
     local = kn_ref[...] - base + HALO
-    basis = spline_basis(ph_ref[...])
-    tables = [jnp.broadcast_to(x_ref[c : c + 1, :], (tiles, LANES)) for c in range(3)]
-    second = first_ref[...]
+    tables = [jnp.broadcast_to(x[c], (tiles, LANES)) for c in range(3)]
+    second = first
     for i in range(4):
         moved = ap_ref[0] * lane_pick(tables[0], local + i)
         for c in range(1, 3):
             moved = moved + ap_ref[c] * lane_pick(tables[c], local + i)
         second = second - basis[i] * moved
     second_ref[...] = second
-    step_ref[...] = x_ref[3:6, 0:nodes_dev]
     weighted = weights * second
     for a in range(CPAR):
-        cal[a * tiles : (a + 1) * tiles, :] = weighted * cp_ref[a]
-    cal[CPAR * tiles :, :] = jnp.zeros(((8 - CPAR) * tiles, LANES), F32)
+        rcal[a * tiles : (a + 1) * tiles, :] = weighted * cp_ref[a]
+    rcal[CPAR * tiles :, :] = jnp.zeros(((8 - CPAR) * tiles, LANES), F32)
     sums = [jnp.sum(weighted * gp_ref[a], axis=0, keepdims=True) for a in range(GPAR)]
-    acc[...] = jnp.zeros_like(acc)
-
-    def step(no, carry):
+    acc_rhs[...] = jnp.zeros_like(acc_rhs)
+
+    def bin_rhs(no, carry):
         tile = no * 2
         units = two_rows(ci_ref, tile)
         upper, lower = lax.shift_right_logical(units, 8), lax.bitwise_and(units, 255)
-        pieces = [by_high(p, upper) for p in split_three(two_tiles(cal, tile, 8, tiles))]
+        pieces = [by_high(p, upper) for p in split_three(two_tiles(rcal, tile, 8, tiles))]
         lhs = jnp.concatenate(pieces, axis=0).astype(BF16)
-        acc[...] = acc[...] + dot_nt(lhs, one_hot(lower, LOW))
+        acc_rhs[...] = acc_rhs[...] + dot_nt(lhs, one_hot(lower, LOW))
         return carry
 
-    lax.fori_loop(0, tiles // 2, step, 0, unroll=2)
+    lax.fori_loop(0, tiles // 2, bin_rhs, 0, unroll=2)
     rows = 8 * (UNITS // LOW)
-    total = acc[0:rows, :] + acc[rows : 2 * rows, :] + acc[2 * rows : 3 * rows, :]
+    total = acc_rhs[0:rows, :] + acc_rhs[rows : 2 * rows, :] + acc_rhs[2 * rows : 3 * rows, :]
     lane = lax.broadcasted_iota(jnp.int32, (1, LANES), 1)
     folded = [row + pltpu.roll(row, LANES // 2, 1) for row in sums]
     packed = [jnp.where(lane < LANES // 2, folded[2 * k], folded[2 * k + 1]) for k in range(2)]
@@ -486,75 +442,84 @@
             for k in range(2):
                 rhs_ref[block, CPAR + k : CPAR + k + 1, 0:LANES] = packed[k]
 
-
-def solve_kernel(
-    shape, rhs_ref, total_ref, out_ref, glob_ref,
-    whole, mine, ready, spread, whole_s, whole_r, mine_s, mine_r, spread_s, spread_r,
-):
-    count, groups, blocks = shape
     width = rhs_ref.shape[2]
-    t, g = lax.axis_index("tm"), lax.axis_index("grp")
     block = lax.rem(t, blocks)
     family = t - block
 
-    def peer_tm(k):
-        return lax.rem(t + k, count)
-
-    def peer_grp(k):
-        return lax.rem(g + k, groups)
-
-    barrier = pltpu.get_barrier_semaphore()
-
-    def greet(where):
-        pl.semaphore_signal(barrier, inc=1, device_id=where, device_id_type=MESH)
-
-    lax.fori_loop(1, count, lambda k, c: (greet({"tm": peer_tm(k), "grp": g}), c)[1], 0)
+    def rwhole_copy(k, slot):
+        p = peer_tm(k)
+        return pltpu.make_async_remote_copy(
+            src_ref=rhs_ref.at[lax.rem(p, blocks)],
+            dst_ref=rwhole.at[slot],
+            send_sem=rwhole_s.at[k],
+            recv_sem=rwhole_r.at[slot],
+            device_id={"tm": p, "grp": g},
+            device_id_type=MESH,
+        )
+
+    lax.fori_loop(1, count, lambda k, c: (rwhole_copy(k, t).start(), c)[1], 0)
+    rwhole[t] = rhs_ref[block]
+    lax.fori_loop(1, count, lambda k, c: (whole_arrival(k).wait_recv(), c)[1], 0)
+    mine[g] = lax.fori_loop(1, count, lambda k, c: c + whole[k], whole[0])
+
+    def mine_copy(k):
+        return pltpu.make_async_remote_copy(
+            src_ref=mine.at[g],
+            dst_ref=mine.at[g],
+            send_sem=mine_s.at[k],
+            recv_sem=mine_r.at[g],
+            device_id={"tm": t, "grp": peer_grp(k)},
+            device_id_type=MESH,
+        )
+
+    def mine_arrival(k):
+        q = peer_grp(k)
+        return pltpu.make_async_remote_copy(
+            src_ref=mine.at[q],
+            dst_ref=mine.at[q],
+            send_sem=mine_s.at[k],
+            recv_sem=mine_r.at[q],
+            device_id={"tm": t, "grp": q},
+            device_id_type=MESH,
+        )
+
     for k in range(1, groups):
-        greet({"tm": t, "grp": peer_grp(k)})
-    pl.semaphore_wait(barrier, count - 1 + groups - 1)
-
-    def whole_copy(k, slot):
-        p = peer_tm(k)
-        return pltpu.make_async_remote_copy(
-            src_ref=rhs_ref.at[lax.rem(p, blocks)],
-            dst_ref=whole.at[slot],
-            send_sem=whole_s.at[k],
-            recv_sem=whole_r.at[slot],
-            device_id={"tm": p, "grp": g},
-            device_id_type=MESH,
-        )
-
-    lax.fori_loop(1, count, lambda k, c: (whole_copy(k, t).start(), c)[1], 0)
-    whole[t] = rhs_ref[block]
-    matrix = [total_ref[p : p + 1, :] for p in range(21)]
+        mine_copy(k).start()
+    for k in range(1, groups):
+        mine_arrival(k).wait_recv()
+    total = mine[0]
+    for q in range(1, groups):
+        total = total + mine[q]
+    unit_total = total
+    matrix = [unit_total[p : p + 1, :] for p in range(21)]
     lower, inverse = cholesky_lists(symmetric(matrix, CPAR), CPAR)
     upper_g = [
         jnp.broadcast_to(
-            jnp.sum(total_ref[21 + p : 22 + p, 0:LANES], axis=1, keepdims=True), (1, LANES)
+            jnp.sum(unit_total[21 + p : 22 + p, 0:LANES], axis=1, keepdims=True), (1, LANES)
         )
         for p in range(10)
     ]
     lower_g, inverse_g = cholesky_lists(symmetric(upper_g, GPAR), GPAR)
-    lax.fori_loop(1, count, lambda k, c: (whole_copy(k, peer_tm(k)).wait_recv(), c)[1], 0)
-    mine[g] = lax.fori_loop(1, count, lambda k, c: c + whole[k], whole[0])
-
-    def mine_copy(k, slot):
-        return pltpu.make_async_remote_copy(
-            src_ref=mine.at[slot],
-            dst_ref=mine.at[slot],
-            send_sem=mine_s.at[k],
-            recv_sem=mine_r.at[slot],
+    lax.fori_loop(1, count, lambda k, c: (rwhole_copy(k, peer_tm(k)).wait_recv(), c)[1], 0)
+    rmine[g] = lax.fori_loop(1, count, lambda k, c: c + rwhole[k], rwhole[0])
+
+    def rmine_copy(k, slot):
+        return pltpu.make_async_remote_copy(
+            src_ref=rmine.at[slot],
+            dst_ref=rmine.at[slot],
+            send_sem=rmine_s.at[k],
+            recv_sem=rmine_r.at[slot],
             device_id={"tm": t, "grp": peer_grp(k)},
             device_id_type=MESH,
         )
 
     for k in range(1, groups):
-        mine_copy(k, g).start()
+        rmine_copy(k, g).start()
     for k in range(1, groups):
-        mine_copy(k, peer_grp(k)).wait_recv()
-    total = mine[0]
+        rmine_copy(k, peer_grp(k)).wait_recv()
+    total = rmine[0]
     for q in range(1, groups):
-        total = total + mine[q]
+        total = total + rmine[q]
     right = [total[c : c + 1, :] for c in range(CPAR)]
     white = solve_lower(lower, inverse, right)
     solved = solve_upper(lower, inverse, white)
@@ -594,10 +559,14 @@
         0,
     )
     out_ref[...] = spread[...]
-    lax.fori_loop(1, count, lambda k, c: (whole_copy(k, t).wait_send(), c)[1], 0)
+    lax.fori_loop(1, count, lambda k, c: (rwhole_copy(k, t).wait_send(), c)[1], 0)
     for k in range(1, groups):
-        mine_copy(k, g).wait_send()
+        rmine_copy(k, g).wait_send()
     lax.fori_loop(1, blocks, lambda k, c: (spread_copy(k, block).wait_send(), c)[1], 0)
+    for k in range(1, groups):
+        mine_copy(k).wait_send()
+    each_near(lambda offset, k: near_copy(offset, k).wait_send())
+    lax.fori_loop(1, count, lambda k, c: (whole_copy(k).wait_send(), c)[1], 0)
 
 
 def final_kernel(
@@ -647,62 +616,42 @@
         return jax.ShapeDtypeStruct(dims, F32)
 
     dma = pltpu.SemaphoreType.DMA
-    first, normals, mats = pl.pallas_call(
-        functools.partial(first_kernel, blocks),
+    second, attitude_step, solved, global_out = pl.pallas_call(
+        functools.partial(step_kernel, shape, nodes_dev),
         out_shape=(
-            out(tiles, LANES), out(NORMAL_ROWS, LANES), out(blocks, NORMAL_ROWS, width),
+            out(tiles, LANES), out(3, nodes_dev), out(blocks, 16, width), out(2 * GPAR, LANES),
         ),
         scratch_shapes=[
             pltpu.VMEM((ATT_ROWS * tiles, LANES), F32),
             pltpu.VMEM((UNIT_ROWS * tiles, LANES), F32),
+            pltpu.VMEM((8 * tiles, LANES), F32),
             pltpu.VMEM((ATT_ROWS, LANES), F32),
             pltpu.VMEM((UNIT_ROWS * (UNITS // LOW), LOW), F32),
-        ],
-        name="first",
-    )(
-        flat(residual), weights, deep(source_part), flat(source_index), deep(source_delta),
-        axes, phase, knots, calib, units, glob,
-    )
-    x, total = pl.pallas_call(
-        functools.partial(attitude_kernel, shape, nodes_dev),
-        out_shape=(out(8, LANES), out(NORMAL_ROWS, width)),
-        scratch_shapes=[
+            pltpu.VMEM((3 * 8 * (UNITS // LOW), LOW), F32),
+            pltpu.VMEM((NORMAL_ROWS, LANES), F32),
+            pltpu.VMEM((blocks, NORMAL_ROWS, width), F32),
+            pltpu.VMEM((blocks, 8, width), F32),
             pltpu.VMEM((3 * groups, NORMAL_ROWS, LANES), F32),
             pltpu.VMEM((groups, NORMAL_ROWS, width), F32),
             pltpu.VMEM((count, NORMAL_ROWS, width), F32),
-            dma((3 * groups,)), dma((3 * groups,)),
-            dma((groups,)), dma((groups,)),
-            dma((count,)), dma((count,)),
-        ],
-        in_specs=[pl.BlockSpec(memory_space=pltpu.VMEM)] * 2,
-        compiler_params=pltpu.CompilerParams(collective_id=0, has_side_effects=True),
-        name="attitude",
-    )(normals, mats)
-    second, rhs, attitude_step = pl.pallas_call(
-        functools.partial(second_kernel, blocks),
-        out_shape=(out(tiles, LANES), out(blocks, 8, width), out(3, nodes_dev)),
-        scratch_shapes=[
-            pltpu.VMEM((8 * tiles, LANES), F32),
-            pltpu.VMEM((3 * 8 * (UNITS // LOW), LOW), F32),
-        ],
-        name="second",
-    )(first, x, weights, axes, phase, knots, calib, units, glob)
-    solved, global_out = pl.pallas_call(
-        functools.partial(solve_kernel, shape),
-        out_shape=(out(blocks, 16, width), out(2 * GPAR, LANES)),
-        scratch_shapes=[
             pltpu.VMEM((count, 8, width), F32),
             pltpu.VMEM((groups, 8, width), F32),
             pltpu.VMEM((16, width), F32),
             pltpu.VMEM((blocks, 16, width), F32),
+            dma((3 * groups,)), dma((3 * groups,)),
+            dma((groups,)), dma((groups,)),
+            dma((count,)), dma((count,)),
             dma((count,)), dma((count,)),
             dma((groups,)), dma((groups,)),
             dma((blocks,)), dma((blocks,)),
         ],
-        in_specs=[pl.BlockSpec(memory_space=pltpu.VMEM)] * 2,
-        compiler_params=pltpu.CompilerParams(collective_id=1, has_side_effects=True),
-        name="solve",
-    )(rhs, total)
+        in_specs=[pl.BlockSpec(memory_space=pltpu.VMEM)] * 11,
+        compiler_params=pltpu.CompilerParams(collective_id=0, has_side_effects=True),
+        name="step",
+    )(
+        flat(residual), weights, deep(source_part), flat(source_index), deep(source_delta),
+        axes, phase, knots, calib, units, glob,
+    )
     final, calib_step = pl.pallas_call(
         functools.partial(final_kernel, blocks),
         out_shape=(out(tiles, LANES), out(CPAR, UNITS)),

time: 48.5 us -> 35.6 us (0.73)
  Pallas kernels: 46.9 us -> 32.8 us
  local copies, waits for them, and re-layouts: 0.63 us -> 1.87 us
    pallas_call x4 -> x1, Pallas kernels: 44.5 us -> 30.5 us  [per_device(): pl.pallas_call(functools.partial(step_kernel, shape, nodes_dev), out_shap...]
    unnamed x2 -> x5, local copies, waits for them, and re-layouts: 0.01 us -> 1.25 us
where the time goes in v1:
time: 35.6 us; the launch traced here: 35.4 us
  Pallas kernels  32.8 us (92%)
  local copies, waits for them, and re-layouts  1.87 us (5%)
  between operations  0.65 us (2%)
    pallas_call x1, Pallas kernels, per_device(): pl.pallas_call(functools.partial(step_kernel, shape, nodes_dev), out_shap...  30.5 us
    pallas_call x1, Pallas kernels, per_device(): pl.pallas_call(functools.partial(final_kernel, blocks), out_shape=(out(ti...  2.36 us
    unnamed x5, local copies, waits for them, and re-layouts  1.25 us

profile of v1, /device:TPU:0, one launch (start us, length us, event | category | flops | bytes accessed | tf_op | source)
XLA Modules:
  0.0 35.4 jit_solution(15883745923366934375)
XLA Ops:
  0.6 30.5 %step.1 = (f32[24,128]{1,0:T(8,128)}, f32[3,96]{1,0:T(4,128)}, f32[16,16,128]{2,1,0:T(8,128)}, f32[8,128]{1,0:T(8,128)}) custom-call(f32[24,128]{1,0:T(8,128)} %bitcast.21, f32[24,128]{1,0:T(8,128)} %bitcast.22, f32[5,24,128]{2,1,0:T(8,128)} %bitcast.17, s32[24,128]{1,0:T(8,128)} %bitcast.23, f32[5,32,128]{2,1,0:T(8,128)} %bitcast.16, ...), custom_call_target="tpu_custom_call" | custom-call | tf_op jit(solution)/shard_map/step/pallas_call | solution.py:619
  31.1 0.0 copy-start
  31.1 2.4 %final.1 = (f32[24,128]{1,0:T(8,128)}, f32[6,2048]{1,0:T(8,128)}) custom-call(f32[24,128]{1,0:T(8,128)} %get-tuple-element.10.second_ref, f32[16,16,128]{2,1,0:T(8,128)} %get-tuple-element.11.solved_ref, f32[8,128]{1,0:T(8,128)} %get-tuple-element.12.glob_ref, f32[6,24,128]{2,1,0:T(8,128)} %bitcast.13, s32[24,128]{1,0:T(8,128)} %bitcast.19, ...), custom_call_target="tpu_custom_call" | custom-call | tf_op jit(solution)/shard_map/final/pallas_call | solution.py:655
  33.5 0.0 copy-done
  33.5 0.6 %slice_reduce_fusion = f32[4]{0:T(128)} fusion(f32[8,128]{1,0:T(8,128)S(1)} %copy-done), kind=kLoop, calls=%fused_computation | loop fusion | bytes 32 | tf_op jit(solution)/shard_map/slice | solution.py:660
  34.1 0.0 copy-start.1
  34.1 0.7 %copy-done.1 = f32[3,96]{1,0:T(4,128)S(1)} copy-done((f32[3,96]{1,0:T(4,128)S(1)}, f32[3,96]{1,0:T(4,128)}, u32[]{:S(2)}) %copy-start.1) | copy-done | bytes 1176
  34.8 0.6 %copy.16 = f32[3,96]{1,0:T(4,128)} copy(f32[3,96]{1,0:T(4,128)S(1)} %copy-done.1) | data formatting | bytes 2304
Async XLA Ops:
  31.1 2.4 %copy-start = (f32[8,128]{1,0:T(8,128)S(1)}, f32[8,128]{1,0:T(8,128)}, u32[]{:S(2)}) copy-start(f32[8,128]{1,0:T(8,128)} %get-tuple-element.12.glob_ref) | copy-start | bytes 12292
  34.1 0.7 %copy-start.1 = (f32[3,96]{1,0:T(4,128)S(1)}, f32[3,96]{1,0:T(4,128)}, u32[]{:S(2)}) copy-start(f32[3,96]{1,0:T(4,128)} %get-tuple-element.21) | copy-start | bytes 3460

commit v2 on v1

--- a/solution.py
+++ b/solution.py
@@ -221,7 +221,7 @@
         acc_att[...] = part
         return carry
 
-    lax.fori_loop(0, tiles // 2, bin_nodes, 0, unroll=2)
+    lax.fori_loop(0, tiles // 2, bin_nodes, 0, unroll=6)
     band = [None] * 5
     place = 0
     for i in range(4):
@@ -301,7 +301,7 @@
         acc_cal[...] = part
         return carry
 
-    lax.fori_loop(0, tiles // 2, bin_units, 0, unroll=2)
+    lax.fori_loop(0, tiles // 2, bin_units, 0, unroll=6)
     mats_ref[...] = jnp.zeros_like(mats_ref)
     for block, at, h, start in block_pieces(blocks):
         mats_ref[block, 0:21, at : at + LANES] = acc_cal[
@@ -426,7 +426,7 @@
         acc_rhs[...] = acc_rhs[...] + dot_nt(lhs, one_hot(lower, LOW))
         return carry
 
-    lax.fori_loop(0, tiles // 2, bin_rhs, 0, unroll=2)
+    lax.fori_loop(0, tiles // 2, bin_rhs, 0, unroll=6)
     rows = 8 * (UNITS // LOW)
     total = acc_rhs[0:rows, :] + acc_rhs[rows : 2 * rows, :] + acc_rhs[2 * rows : 3 * rows, :]
     lane = lax.broadcasted_iota(jnp.int32, (1, LANES), 1)
@@ -570,8 +570,15 @@
 
 
 def final_kernel(
-    blocks, second_ref, solved_ref, glob_ref, cp_ref, ci_ref, gp_ref, res_ref, step_ref
+    blocks, second_ref, solved_ref, glob_ref, att_ref, cp_ref, ci_ref, gp_ref,
+    res_ref, att_out_ref, step_ref, glob_out_ref,
 ):
+    att_out_ref[...] = att_ref[...]
+    lane = lax.broadcasted_iota(jnp.int32, (1, LANES), 1)
+    packed = jnp.zeros((1, LANES), F32)
+    for c in range(GPAR):
+        packed = jnp.where(lane == c, glob_ref[c : c + 1, :], packed)
+    glob_out_ref[...] = packed[:, 0:GPAR]
     tiles = second_ref.shape[0]
     units = ci_ref[...]
     high, low = lax.shift_right_logical(units, 7), lax.bitwise_and(units, 127)
@@ -652,12 +659,14 @@
         flat(residual), weights, deep(source_part), flat(source_index), deep(source_delta),
         axes, phase, knots, calib, units, glob,
     )
-    final, calib_step = pl.pallas_call(
+    final, attitude_out, calib_step, global_step = pl.pallas_call(
         functools.partial(final_kernel, blocks),
-        out_shape=(out(tiles, LANES), out(CPAR, UNITS)),
+        out_shape=(
+            out(tiles, LANES), out(3, nodes_dev), out(CPAR, UNITS), out(1, GPAR),
+        ),
         name="final",
-    )(second, solved, global_out, calib, units, glob)
-    return final.reshape(residual.shape), attitude_step, calib_step, global_out[:GPAR, 0]
+    )(second, solved, global_out, attitude_step, calib, units, glob)
+    return final.reshape(residual.shape), attitude_out, calib_step, global_step.reshape(GPAR)
 
 
 def solution(mesh):

time: 35.6 us -> 33.1 us (0.930)
  local copies, waits for them, and re-layouts: 1.87 us -> 0 us
  Pallas kernels: 32.8 us -> 32.3 us
    unnamed x5 -> x0, local copies, waits for them, and re-layouts: 1.25 us -> none
    pallas_call x1, Pallas kernels: 30.5 us -> 29.9 us  [per_device(): pl.pallas_call(functools.partial(step_kernel, shape, nodes_dev), out_shap...]
    slice x1 -> x0, local copies, waits for them, and re-layouts: 0.63 us -> none  [per_device(): global_out[:GPAR, 0]]
where the time goes in v2:
time: 33.1 us; the launch traced here: 32.9 us
  Pallas kernels  32.3 us (98%)
  between operations  0.64 us (2%)
    pallas_call x1, Pallas kernels, per_device(): pl.pallas_call(functools.partial(step_kernel, shape, nodes_dev), out_shap...  29.9 us
    pallas_call x1, Pallas kernels, per_device(): pl.pallas_call(functools.partial(final_kernel, blocks), out_shape=(out(ti...  2.4 us

profile of v2, /device:TPU:0, one launch (start us, length us, event | category | flops | bytes accessed | tf_op | source)
XLA Modules:
  0.0 32.9 jit_solution(2459827685905155834)
XLA Ops:
  0.6 29.9 %step.1 = (f32[24,128]{1,0:T(8,128)}, f32[3,96]{1,0:T(4,128)}, f32[16,16,128]{2,1,0:T(8,128)}, f32[8,128]{1,0:T(8,128)}) custom-call(f32[24,128]{1,0:T(8,128)} %bitcast.22, f32[24,128]{1,0:T(8,128)} %bitcast.23, f32[5,24,128]{2,1,0:T(8,128)} %bitcast.18, s32[24,128]{1,0:T(8,128)} %bitcast.24, f32[5,32,128]{2,1,0:T(8,128)} %bitcast.17, ...), custom_call_target="tpu_custom_call" | custom-call | tf_op jit(solution)/shard_map/step/pallas_call | solution.py:626
  30.5 2.4 %final.1 = (f32[24,128]{1,0:T(8,128)}, f32[3,96]{1,0:T(4,128)}, f32[6,2048]{1,0:T(8,128)}, f32[1,4]{1,0:T(1,128)}) custom-call(f32[24,128]{1,0:T(8,128)} %get-tuple-element.12.second_ref, f32[16,16,128]{2,1,0:T(8,128)} %get-tuple-element.13.solved_ref, f32[8,128]{1,0:T(8,128)} %get-tuple-element.14.glob_ref, f32[3,96]{1,0:T(4,128)} %get-tuple-element.15.att_ref, ...), custom_call_target="tpu_custom_call" | custom-call | tf_op jit(solution)/shard_map/final/pallas_call | solution.py:662
